TPU v7x, 8 devices: a whole 2x2x1 slice. The times are simulated.
8 devices in a mesh: tp: 2 (over z, y), dp: 4 (over x, core).
Axes of the slice: x: 2, y: 2, z: 1, core: 2. Of those that a mesh axis runs over, the one named last changes fastest.
Arguments:
- x_in: bfloat16 [32, 512, 3840], P('dp')
- dy_in: bfloat16 [32, 512, 3840], P('dp')
- positions: int32 [32, 512], P('dp')
- g_attn: bfloat16 [3840], replicated
- q_gain: bfloat16 [256], replicated
- k_gain: bfloat16 [256], replicated
- w_q: bfloat16 [3840, 4096], P(None, 'tp')
- w_k: bfloat16 [3840, 2048], P(None, 'tp')
- w_v: bfloat16 [3840, 2048], P(None, 'tp')
- w_o: bfloat16 [4096, 3840], P('tp')
Outputs:
- output 1: bfloat16 [32, 512, 3840], P('dp')
- output 2: bfloat16 [32, 512, 3840], P('dp')
- output 3: float32 [3840, 4096], P(None, 'tp')
- output 4: float32 [3840, 2048], P(None, 'tp')
- output 5: float32 [3840, 2048], P(None, 'tp')
- output 6: float32 [4096, 3840], P('tp')
- output 7: float32 [256], replicated
- output 8: float32 [256], replicated
- output 9: float32 [3840], replicated
All inputs are finite; a program needn't handle non-finite values.
Results may differ from a plain program's by a relative error of at most 0.0184639.
Values sent between devices are 32-bit elements.
A program may use at most 1 GiB of HBM per device.

v0:
```python
import jax
import jax.numpy as jnp
from jax import lax
from jax.sharding import PartitionSpec as P

EPS = 1e-6
ROPE_THETA = 1000000.0


def rope_tables(positions, head_dim):
    inv_freq = ROPE_THETA ** (-jnp.arange(0, head_dim, 2, dtype=jnp.float32) / head_dim)
    angles = positions.astype(jnp.float32)[:, :, None, None] * inv_freq
    return jnp.cos(angles), jnp.sin(angles)


def head_norm_rope(t_proj, weight, cos_tab, sin_tab):
    t_f32 = t_proj.astype(jnp.float32)
    t_hat = t_f32 * lax.rsqrt(jnp.mean(t_f32 * t_f32, axis=-1, keepdims=True) + EPS)
    scaled = t_hat * weight
    half_dim = scaled.shape[-1] // 2
    low_half = scaled[..., :half_dim]
    high_half = scaled[..., half_dim:]
    return jnp.concatenate([low_half * cos_tab - high_half * sin_tab, high_half * cos_tab + low_half * sin_tab], axis=-1)


def attention_pair(q_rot, k_rot, v_proj, d_out):
    n_batch, n_seq, n_kv, head_dim = k_rot.shape
    group_size = q_rot.shape[2] // n_kv
    q_grp = q_rot.reshape(n_batch, n_seq, n_kv, group_size, head_dim)
    do_grp = d_out.reshape(n_batch, n_seq, n_kv, group_size, head_dim)
    att_scale = head_dim ** -0.5
    scores = jnp.einsum("bqkgd,bskd->bkgqs", q_grp, k_rot, preferred_element_type=jnp.float32) * att_scale
    causal = jnp.arange(n_seq)[:, None] >= jnp.arange(n_seq)[None, :]
    attn_prob = jax.nn.softmax(jnp.where(causal, scores, -jnp.inf), axis=-1)
    prob_bf = attn_prob.astype(jnp.bfloat16)
    attn_out = jnp.einsum("bkgqs,bskd->bqkgd", prob_bf, v_proj, preferred_element_type=jnp.float32).astype(jnp.bfloat16)
    d_val = jnp.einsum("bkgqs,bqkgd->bskd", prob_bf, do_grp, preferred_element_type=jnp.float32).astype(jnp.bfloat16)
    d_prob = jnp.einsum("bqkgd,bskd->bkgqs", do_grp, v_proj, preferred_element_type=jnp.float32)
    d_score = (attn_prob * (d_prob - jnp.sum(d_prob * attn_prob, axis=-1, keepdims=True)) * att_scale).astype(jnp.bfloat16)
    d_query = jnp.einsum("bkgqs,bskd->bqkgd", d_score, k_rot, preferred_element_type=jnp.float32).astype(jnp.bfloat16)
    d_key = jnp.einsum("bkgqs,bqkgd->bskd", d_score, q_grp, preferred_element_type=jnp.float32).astype(jnp.bfloat16)
    return attn_out.reshape(q_rot.shape), d_query.reshape(q_rot.shape), d_key, d_val


def solution(mesh):
    tok_spec = P("dp", None, None)
    col_spec = P(None, "tp")
    row_spec = P("tp", None)

    def per_device(x_in, dy_in, positions, g_attn, q_gain, k_gain, w_q, w_k, w_v, w_o):
        n_batch, n_seq, n_dim = x_in.shape
        head_dim = q_gain.shape[0]
        n_heads = w_q.shape[1] // head_dim
        n_kv = w_k.shape[1] // head_dim
        x_f32 = x_in.astype(jnp.float32).reshape(-1, n_dim)
        inv_rms = lax.rsqrt(jnp.mean(x_f32 * x_f32, axis=-1, keepdims=True) + EPS)
        x_hat = x_f32 * inv_rms
        normed = (x_hat * g_attn.astype(jnp.float32)).astype(jnp.bfloat16)
        q_raw = jnp.dot(normed, w_q, preferred_element_type=jnp.float32).astype(jnp.bfloat16).reshape(n_batch, n_seq, n_heads, head_dim)
        k_raw = jnp.dot(normed, w_k, preferred_element_type=jnp.float32).astype(jnp.bfloat16).reshape(n_batch, n_seq, n_kv, head_dim)
        v_proj = jnp.dot(normed, w_v, preferred_element_type=jnp.float32).astype(jnp.bfloat16).reshape(n_batch, n_seq, n_kv, head_dim)
        cos_tab, sin_tab = rope_tables(positions, head_dim)
        q_rot, q_pull = jax.vjp(lambda t_proj, weight: head_norm_rope(t_proj, weight, cos_tab, sin_tab), q_raw, q_gain.astype(jnp.float32))
        k_rot, k_pull = jax.vjp(lambda t_proj, weight: head_norm_rope(t_proj, weight, cos_tab, sin_tab), k_raw, k_gain.astype(jnp.float32))
        dy_flat = dy_in.reshape(-1, n_dim)
        d_out = jnp.einsum("td,id->ti", dy_flat, w_o, preferred_element_type=jnp.float32).astype(jnp.bfloat16).reshape(n_batch, n_seq, n_heads, head_dim)
        attn_out, dq_rot, dk_rot, dv_proj = attention_pair(q_rot.astype(jnp.bfloat16), k_rot.astype(jnp.bfloat16), v_proj, d_out)
        o_flat = attn_out.reshape(-1, n_heads * head_dim)
        attn_sum = lax.psum(jnp.dot(o_flat, w_o, preferred_element_type=jnp.float32), "tp")
        y_out = (x_f32 + attn_sum).astype(jnp.bfloat16).reshape(x_in.shape)
        dw_o = lax.psum(jnp.einsum("ti,td->id", o_flat, dy_flat, preferred_element_type=jnp.float32), "dp")
        dq_raw, dq_part = q_pull(dq_rot.astype(jnp.float32))
        dk_raw, dk_part = k_pull(dk_rot.astype(jnp.float32))
        dq_flat = dq_raw.reshape(-1, n_heads * head_dim)
        dk_flat = dk_raw.reshape(-1, n_kv * head_dim)
        dv_flat = dv_proj.reshape(-1, n_kv * head_dim)
        dw_q = lax.psum(jnp.einsum("td,ti->di", normed, dq_flat, preferred_element_type=jnp.float32), "dp")
        dw_k = lax.psum(jnp.einsum("td,ti->di", normed, dk_flat, preferred_element_type=jnp.float32), "dp")
        dw_v = lax.psum(jnp.einsum("td,ti->di", normed, dv_flat, preferred_element_type=jnp.float32), "dp")
        d_part = (jnp.einsum("ti,di->td", dq_flat, w_q, preferred_element_type=jnp.float32) + jnp.einsum("ti,di->td", dk_flat, w_k, preferred_element_type=jnp.float32) + jnp.einsum("ti,di->td", dv_flat, w_v, preferred_element_type=jnp.float32))
        d_normed = lax.psum(d_part, "tp")
        dq_gain = lax.psum(dq_part, ("tp", "dp"))
        dk_gain = lax.psum(dk_part, ("tp", "dp"))
        dg_attn = lax.psum(jnp.sum(d_normed * x_hat, axis=0), "dp")
        d_scaled = d_normed * g_attn.astype(jnp.float32)
        dx_f32 = dy_flat.astype(jnp.float32) + inv_rms * (d_scaled - x_hat * jnp.mean(d_scaled * x_hat, axis=-1, keepdims=True))
        dx_out = dx_f32.astype(jnp.bfloat16).reshape(x_in.shape)
        return y_out, dx_out, dw_q, dw_k, dw_v, dw_o, dq_gain, dk_gain, dg_attn

    return jax.shard_map(per_device, mesh=mesh, in_specs=(tok_spec, tok_spec, P("dp", None), P(), P(), P(), col_spec, col_spec, col_spec, row_spec), out_specs=(tok_spec, tok_spec, col_spec, col_spec, col_spec, row_spec, P(), P(), P()), check_vma=False)
```

profile of v0, /device:TPU:0, one launch (start us, length us, event | category | flops | bytes accessed | tf_op | source)
XLA Modules:
  0.0 5745.5 jit_solution(4271794002250544040)
XLA Ops:
  26.0 73.3 %convolution_convert_fusion = bf16[4096,2048]{1,0:T(8,128)(2,1)} fusion(bf16[4096,3840]{1,0:T(8,128)(2,1)} %bitcast.205, bf16[2048,3840]{1,0:T(8,128)(2,1)} %param.19), kind=kOutput, calls=%fused_computation.70 | convolution fusion | flops 64432898048 | bytes 63963136 | tf_op jit(solution)/shard_map/td,id->ti/dot_general | solution.py:66
  99.3 27.7 reshape_reshape.7
  127.0 40.8 copy.159
  167.8 21.9 fusion.9
  189.6 39.8 convolution_convert_fusion.1
  229.4 14.5 reshape.170
  243.9 41.3 convert_convert_fusion.2
  285.2 20.4 reshape.177
  316.9 75.3 %convert_convert_fusion.1 = f32[4096,2048]{1,0:T(8,128)} fusion(bf16[4096,3840]{1,0:T(8,128)(2,1)} %fusion.9, bf16[3840,2048]{1,0:T(8,128)(2,1)} %param.16), kind=kOutput, calls=%fused_computation.67 | convolution fusion | flops 64441286656 | bytes 80740352 | tf_op jit(solution)/shard_map/dot_general | solution.py:59
  392.2 20.0 copy.183
  455.2 23.9 fusion.27
  479.1 17.2 subtract_convert_fusion
  514.5 31.0 fusion.41
  545.5 31.6 fusion.36
  577.1 66.2 %fusion.59 = (f32[8,4,2,512]{3,2,1,0:T(2,128)S(1)}, f32[8,4,2,512,512]{3,4,2,1,0:T(8,128)}) fusion(f32[8,4,512,512,2]{3,2,4,1,0:T(8,128)} %fusion.36, pred[512,512]{0,1:T(8,128)(4,1)S(1)} %copy-done.17), kind=kOutput, calls=%fused_computation.107 | output fusion | flops 100663808 | bytes 134610944 | tf_op jit(solution)/shard_map/sub | solution.py:34
  643.3 34.3 fusion.39
  677.6 91.7 %convert_bitcast_fusion = f32[8,512,4,256]{3,1,2,0:T(8,128)} fusion(bf16[8,512,4,2,128]{4,1,3,2,0:T(8,128)(2,1)} %bitcast.201, bf16[8,512,4,2,128]{4,1,3,2,0:T(8,128)(2,1)} %bitcast.199, f32[8,4,512,512,2]{3,2,4,1,0:T(8,128)} %fusion.41, f32[8,4,2,512,512]{3,4,2,1,0:T(8,128)} %get-tuple-element.40, f32[8,4,2,512]{3,2,1,0:T(2,128)S(1)} %get-tuple-element.39), kind=kOutput, calls=%fused_computation.53 | convolution fusion | flops 8749350912 | bytes 167903232 | tf_op jit(solution)/shard_map/bkgqs,bqkgd->bskd/dot_general | solution.py:41
  769.3 95.5 %convert_convert_fusion = f32[8,4,256,2,512]{4,2,3,1,0:T(8,128)} fusion(f32[8,4,512,512,2]{3,2,4,1,0:T(8,128)} %fusion.41, bf16[8,512,4,128]{3,1,2,0:T(8,128)(2,1)} %get-tuple-element.34, bf16[8,512,4,128]{3,1,2,0:T(8,128)(2,1)} %get-tuple-element.33, f32[8,4,2,512,512]{3,4,2,1,0:T(8,128)} %get-tuple-element.40, f32[8,4,2,512]{3,2,1,0:T(2,128)S(1)} %get-tuple-element.39), kind=kOutput, calls=%fused_computation.59 | convolution fusion | flops 8740962304 | bytes 176291840 | tf_op jit(solution)/shard_map/bkgqs,bskd->bqkgd/dot_general | solution.py:40
  864.8 33.0 convert_bitcast_fusion.1
  921.8 15.7 copy.142
  948.0 21.7 fusion.58
  969.7 17.5 copy.180
  987.2 13.5 multiply_add_fusion.3
  1000.7 17.1 multiply_reduce_fusion.1
  1026.4 14.9 copy.158
  1053.6 17.3 copy.181
  1071.0 22.8 multiply_add_fusion.1
  1093.8 23.8 multiply_reduce_fusion
  1121.7 28.3 fusion.21
  1150.0 16.1 copy.185
  1166.1 76.6 %fusion.60 = f32[4096,3840]{1,0:T(8,128)} fusion(bf16[4096,2048]{0,1:T(8,128)(2,1)} %bitcast.209, bf16[2048,3840]{1,0:T(8,128)(2,1)} %param.19), kind=kOutput, calls=%fused_computation.108 | convolution fusion | flops 64424509440 | bytes 95420416 | tf_op jit(solution)/shard_map/dot_general | solution.py:69
  1242.7 44.7 fusion.62
  1287.4 42.2 fusion.61
  1329.6 88.3 %add_add_fusion = f32[4096,3840]{1,0:T(8,128)} fusion(f32[4096,3840]{1,0:T(8,128)} %fusion.62, f32[4096,3840]{1,0:T(8,128)} %fusion.61, bf16[4096,2048]{1,0:T(8,128)(2,1)} %bitcast.211, bf16[3840,2048]{1,0:T(8,128)(2,1)} %param.16), kind=kOutput, calls=%fused_computation.28 | convolution fusion | flops 64455966720 | bytes 221249536 | tf_op jit(solution)/shard_map/ti,di->td/dot_general | solution.py:80
  1418.6 22.1 fusion.18
  1440.7 40.6 fusion.64
  1481.3 38.5 fusion.65
  1519.8 75.1 %fusion.66 = f32[2048,3840]{1,0:T(8,128)} fusion(bf16[4096,2048]{0,1:T(8,128)(2,1)} %bitcast.210, bf16[4096,3840]{1,0:T(8,128)(2,1)} %bitcast.206), kind=kOutput, calls=%fused_computation.114 | convolution fusion | flops 64424509440 | bytes 79691776 | tf_op jit(solution)/shard_map/ti,td->id/dot_general | solution.py:71
  1594.9 76.2 %fusion.63 = f32[3840,2048]{1,0:T(8,128)} fusion(bf16[4096,3840]{1,0:T(8,128)(2,1)} %bitcast.204, bf16[4096,2048]{1,0:T(8,128)(2,1)} %bitcast.212), kind=kOutput, calls=%fused_computation.111 | convolution fusion | flops 64424509440 | bytes 79691776 | tf_op jit(solution)/shard_map/td,ti->di/dot_general | solution.py:77
  1671.8 25.7 all-reduce.4
  1697.5 2434.1 %all-reduce.12.cloned.1.call-done = (f32[4096,3840]{1,0:T(8,128)}, f32[4096,3840]{1,0:T(8,128)}) async-done(((f32[4096,3840]{1,0:T(8,128)}, f32[4096,3840]{1,0:T(8,128)}), (f32[4096,3840]{1,0:T(8,128)}, f32[4096,3840]{1,0:T(8,128)})) %all-reduce.12.cloned.1.call-update) | async-done | bytes 125829136 | tf_op jit(solution)/shard_map/psum | solution.py:69
  4131.6 29.3 fusion.15
  4173.6 79.7 %fusion.14 = (bf16[4096,3840]{1,0:T(8,128)(2,1)}, bf16[4096,3840]{1,0:T(8,128)(2,1)}) fusion(bf16[8,512,3840]{2,1,0:T(8,128)(2,1)} %param.10, f32[4096,3840]{1,0:T(8,128)} %get-tuple-element.22, f32[4096]{0:T(1024)S(1)} %broadcast_multiply_fusion, f32[3840]{0:T(1024)S(1)} %copy-done.14, f32[4096]{0:T(1024)S(1)} %bitcast.221, ...), kind=kLoop, calls=%fused_computation.22 | loop fusion | flops 173015040 | bytes 251706368 | tf_op jit(solution)/shard_map/convert_element_type | solution.py:87
  4253.3 1411.7 %all-reduce.10.cloned.1.call-done = (f32[3840,2048]{1,0:T(8,128)}, f32[3840,1024]{1,0:T(8,128)}, f32[3840,1024]{1,0:T(8,128)}, f32[2048,3840]{1,0:T(8,128)}) async-done(((f32[3840,2048]{1,0:T(8,128)}, f32[3840,1024]{1,0:T(8,128)}, f32[3840,1024]{1,0:T(8,128)}, f32[2048,3840]{1,0:T(8,128)}), (f32[3840,2048]{1,0:T(8,128)}, f32[3840,1024]{1,0:T(8,128)}, f32[3840,1024]{1,0:T(8,128)}, ...) | async-done | bytes 94371856 | tf_op jit(solution)/shard_map/psum | solution.py:77
  5665.0 22.2 copy.206
  5687.2 14.8 copy.207
  5702.0 14.8 copy.208
  5716.9 21.6 copy.209
  (106 shorter events, 164.8 us)
Async XLA Ops:
  7.2 4124.4 %all-reduce.12.cloned.1.call-start = ((), (), s32[]{:S(2)}) async-start(), calls=%async_computation.1 | async-start | bytes 251658240 | tf_op jit(solution)/shard_map/psum | solution.py:69
  127.0 40.8 copy-start.12
  127.0 40.8 copy-start.15
  316.2 76.0 %copy-start.10 = (f32[8,512,4]{1,0,2:T(8,128)}, f32[8,512,4]{1,0,2:T(8,128)S(1)}, u32[]{:S(2)}) copy-start(f32[8,512,4]{1,0,2:T(8,128)S(1)} %copy.133) | copy-start | bytes 196612
  412.3 11.1 copy-start
  423.3 8.5 copy-start.19
  423.3 8.5 copy-start.26
  423.3 15.8 copy-start.20
  429.2 0.7 copy-start.7
  439.2 40.0 copy-start.2
  439.2 40.0 copy-start.4
  450.7 4.5 copy-start.22
  545.5 31.6 copy-start.17
  969.7 17.5 copy-start.3
  987.2 13.5 copy-start.9
  987.2 13.5 copy-start.21
  987.2 30.7 slice-start
  987.2 30.7 slice-start.1
  987.2 30.7 slice-start.2
  1000.7 17.1 copy-start.11
  1000.7 17.2 slice-start.3
  1000.7 17.2 copy-start.1
  1071.0 22.8 copy-start.23
  1093.7 25.9 copy-start.8
  1093.7 27.9 copy-start.5
  1242.7 44.7 copy-start.6
  1417.9 0.7 copy-start.13
  1417.9 0.7 copy-start.18
  1417.9 4247.1 %all-reduce.10.cloned.1.call-start = ((), (), s32[]{:S(2)}) async-start(), calls=%async_computation | async-start | bytes 188743680 | tf_op jit(solution)/shard_map/psum | solution.py:77
  1418.6 62.7 %slice-start.4 = ((s8[8388608]{0:T(1024)(128)(4,1)}), s8[4194304]{0:T(1024)(128)(4,1)S(1)}, s32[]{:S(2)}) async-start(s8[8388608]{0:T(1024)(128)(4,1)} %bitcast.214), calls=%async_computation.6 | async-start | bytes 8388608
  1440.7 40.6 slice-start.5
  1671.1 0.7 copy-start.24
  1671.1 0.7 copy-start.25
  1671.1 2460.5 %copy-start.14 = (f32[3840]{0:T(1024)S(1)}, f32[3840]{0:T(1024)}, u32[]{:S(2)}) copy-start(f32[3840]{0:T(1024)} %convert_element_type.110) | copy-start | bytes 46084
  1671.1 2460.5 %copy-start.16 = (f32[1,4,8,128]{3,1,2,0:T(4,128)S(1)}, f32[1,4,8,128]{3,1,2,0:T(4,128)}, u32[]{:S(2)}) copy-start(f32[1,4,8,128]{3,1,2,0:T(4,128)} %copy.182) | copy-start | bytes 49156
Sparse Core Ops, SparseCore 0:
  1418.0 2713.5 all-reduce.11
  4134.9 1529.9 all-reduce.9
where the time goes:
time: 5760 us; the launch traced here: 5750 us
  waiting for transfers between devices  3850 us (67%)
  matrix products  1030 us (18%)
  other arithmetic  431 us (7%)
  local copies, waits for them, and re-layouts  387 us (7%)
    psum x1, waiting for transfers between devices, per_device(): lax.psum(jnp.dot(o_flat, w_o, preferred_element_type=jnp.float32), 'tp')  2430 us
    psum x1, waiting for transfers between devices, per_device(): lax.psum(jnp.einsum('td,ti->di', normed, dq_flat, preferred_element_type=...  1410 us
    unnamed x78, local copies, waits for them, and re-layouts  193 us
  transfers between devices with their start and end apart: 2, of which 2 were waited for; matrix products, arithmetic and copies ran while one was open for 6% of the time, Pallas kernels for 0%

commit v1 on v0

v1 whole, which is shorter than its diff:
```python
import functools

import jax
import jax.numpy as jnp
from jax import lax
from jax.experimental import pallas as pl
from jax.experimental.pallas import tpu as pltpu
from jax.sharding import PartitionSpec as P


EPS = 1e-6
ROPE_THETA = 1000000.0
LOG2_E = 1.4426950408889634
Q_BLOCK = 256

SWAP_TP = [(0, 1), (1, 0)]


def head_norm(t_raw, eps_dim):
    t_f32 = t_raw.astype(jnp.float32)
    inv = lax.rsqrt(jnp.sum(t_f32 * t_f32, axis=-1, keepdims=True) * (1.0 / eps_dim) + EPS)
    return t_f32 * inv, inv


def rope(u, cos, sin):
    half = u.shape[-1] // 2
    low, high = u[:, :half], u[:, half:]
    return jnp.concatenate([low * cos - high * sin, high * cos + low * sin], axis=-1)


def unrope(g, cos, sin):
    half = g.shape[-1] // 2
    low, high = g[:, :half], g[:, half:]
    return jnp.concatenate([low * cos + high * sin, high * cos - low * sin], axis=-1)


def norm_pull(d_rot, t_hat, inv, gain, cos, sin):
    d_u = unrope(d_rot.astype(jnp.float32), cos, sin)
    by_gain = d_u * t_hat
    d_gain = jnp.sum(by_gain.reshape(-1, 8, by_gain.shape[-1]), axis=0)
    d_hat = d_u * gain
    mean = jnp.sum(d_hat * t_hat, axis=-1, keepdims=True) * (1.0 / t_hat.shape[-1])
    return (inv * (d_hat - t_hat * mean)).astype(jnp.bfloat16), d_gain


def attend(group, dim, qkv_ref, do_ref, cos_ref, sin_ref, qg_ref, kg_ref, o_ref, d_ref, gq_ref, gk_ref, dv_acc, dk_acc):
    seq = qkv_ref.shape[0]
    scale = dim ** -0.5
    cos, sin = cos_ref[...], sin_ref[...]
    q_gain, k_gain = qg_ref[...], kg_ref[...]
    k_hat, k_inv = head_norm(qkv_ref[:, group * dim:(group + 1) * dim], dim)
    k_rot = rope(k_hat * k_gain, cos, sin).astype(jnp.bfloat16)
    v = qkv_ref[:, (group + 1) * dim:]
    nt = (((1,), (1,)), ((), ()))
    tn = (((0,), (0,)), ((), ()))
    dot = functools.partial(lax.dot_general, preferred_element_type=jnp.float32)
    d_gain_q = jnp.zeros((8, dim), jnp.float32)
    dv_acc[...] = jnp.zeros_like(dv_acc)
    dk_acc[...] = jnp.zeros_like(dk_acc)
    for head in range(group):
        cols = slice(head * dim, (head + 1) * dim)
        q_hat, q_inv = head_norm(qkv_ref[:, cols], dim)
        q_rot = rope(q_hat * q_gain, cos, sin).astype(jnp.bfloat16)
        d_out = do_ref[:, cols]
        parts = []
        for start in range(0, seq, Q_BLOCK):
            stop = start + Q_BLOCK
            q_blk, do_blk = q_rot[start:stop], d_out[start:stop]
            s = dot(k_rot[:stop], q_blk, nt)
            key = lax.broadcasted_iota(jnp.int32, s.shape, 0)
            query = lax.broadcasted_iota(jnp.int32, s.shape, 1) + start
            s = jnp.where(key <= query, s, -jnp.inf)
            e = jnp.exp2((s - jnp.max(s, axis=0, keepdims=True)) * (scale * LOG2_E))
            prob = e * (1.0 / jnp.sum(e, axis=0, keepdims=True))
            prob_bf = prob.astype(jnp.bfloat16)
            d_prob = dot(v[:stop], do_blk, nt)
            row = jnp.sum(prob * d_prob, axis=0, keepdims=True)
            d_score = (prob * (d_prob - row) * scale).astype(jnp.bfloat16)
            o_ref[start:stop, cols] = dot(prob_bf, v[:stop], tn).astype(jnp.bfloat16)
            parts.append(dot(d_score, k_rot[:stop], tn).astype(jnp.bfloat16))
            dv_acc[:stop] += lax.dot(prob_bf, do_blk, preferred_element_type=jnp.float32)
            dk_acc[:stop] += lax.dot(d_score, q_blk, preferred_element_type=jnp.float32)
        d_raw, d_gain = norm_pull(jnp.concatenate(parts, axis=0), q_hat, q_inv, q_gain, cos, sin)
        d_ref[:, cols] = d_raw
        d_gain_q += d_gain
    dk_raw, d_gain_k = norm_pull(dk_acc[...].astype(jnp.bfloat16), k_hat, k_inv, k_gain, cos, sin)
    d_ref[:, group * dim:(group + 1) * dim] = dk_raw
    d_ref[:, (group + 1) * dim:] = dv_acc[...].astype(jnp.bfloat16)
    gq_ref[...] = d_gain_q
    gk_ref[...] = d_gain_k


def attention(qkv, d_out, cos, sin, q_gain, k_gain, seq, group, dim):
    rows = qkv.shape[0] // seq
    width = (group + 2) * dim
    kv = qkv.shape[1] // width
    by_head = lambda b, h: (b, h)
    by_row = lambda b, h: (b, 0)
    whole = lambda b, h: (0, 0)
    steps = rows * kv
    flops = 6 * 2 * steps * group * seq * seq * dim * 3 // 4
    return pl.pallas_call(
        functools.partial(attend, group, dim),
        grid=(rows, kv),
        in_specs=[
            pl.BlockSpec((seq, width), by_head),
            pl.BlockSpec((seq, group * dim), by_head),
            pl.BlockSpec((seq, dim // 2), by_row),
            pl.BlockSpec((seq, dim // 2), by_row),
            pl.BlockSpec((1, dim), whole),
            pl.BlockSpec((1, dim), whole),
        ],
        out_specs=[
            pl.BlockSpec((seq, group * dim), by_head),
            pl.BlockSpec((seq, width), by_head),
            pl.BlockSpec((8, dim), by_head),
            pl.BlockSpec((8, dim), by_head),
        ],
        out_shape=[
            jax.ShapeDtypeStruct(d_out.shape, jnp.bfloat16),
            jax.ShapeDtypeStruct(qkv.shape, jnp.bfloat16),
            jax.ShapeDtypeStruct((rows * 8, kv * dim), jnp.float32),
            jax.ShapeDtypeStruct((rows * 8, kv * dim), jnp.float32),
        ],
        scratch_shapes=[pltpu.VMEM((seq, dim), jnp.float32), pltpu.VMEM((seq, dim), jnp.float32)],
        compiler_params=pltpu.CompilerParams(dimension_semantics=("arbitrary", "arbitrary"), vmem_limit_bytes=48 * 1024 * 1024),
        cost_estimate=pl.CostEstimate(flops=flops, bytes_accessed=2 * (qkv.size + d_out.size) * 2, transcendentals=steps * group * seq * seq),
        name="attend",
    )(qkv, d_out, cos, sin, q_gain, k_gain)


def interleave(w_q, w_k, w_v, groups, group, dim):
    cols = []
    for g in groups:
        cols += [w_q[:, g * group * dim:(g + 1) * group * dim], w_k[:, g * dim:(g + 1) * dim], w_v[:, g * dim:(g + 1) * dim]]
    return jnp.concatenate(cols, axis=1)


def dot_nn(a, b):
    return jnp.dot(a, b, preferred_element_type=jnp.float32)


def dot_nt(a, b):
    return jnp.einsum("td,id->ti", a, b, preferred_element_type=jnp.float32)


def dot_tn(a, b):
    return jnp.einsum("td,ti->di", a, b, preferred_element_type=jnp.float32)


def fetch_half(w, core):
    half = w.shape[0] // 2
    send = lax.dynamic_slice_in_dim(w, core * half, half, 0).astype(jnp.float32)
    return lax.ppermute(send, "tp", SWAP_TP)


def join_body(core_ref, near_ref, far_ref, full_ref):
    mine = pl.program_id(0) == core_ref[0]

    @pl.when(mine)
    def _():
        full_ref[...] = near_ref[...].astype(full_ref.dtype)

    @pl.when(jnp.logical_not(mine))
    def _():
        full_ref[...] = far_ref[...].astype(full_ref.dtype)


JOIN_ROWS = 128


def join_halves(near, core, core_swap):
    far = lax.ppermute(near, "dp", core_swap)
    half, width = near.shape
    blocks = half // JOIN_ROWS
    return pl.pallas_call(
        join_body,
        grid_spec=pltpu.PrefetchScalarGridSpec(
            num_scalar_prefetch=1,
            grid=(2, blocks),
            in_specs=[
                pl.BlockSpec((JOIN_ROWS, width), lambda h, i, c: (jnp.where(h == c[0], i, 0), 0)),
                pl.BlockSpec((JOIN_ROWS, width), lambda h, i, c: (jnp.where(h == c[0], 0, i), 0)),
            ],
            out_specs=pl.BlockSpec((JOIN_ROWS, width), lambda h, i, c: (h * blocks + i, 0)),
        ),
        out_shape=jax.ShapeDtypeStruct((2 * half, width), jnp.bfloat16),
        compiler_params=pltpu.CompilerParams(dimension_semantics=("arbitrary", "arbitrary")),
        cost_estimate=pl.CostEstimate(flops=2 * half * width * 32, bytes_accessed=12 * half * width, transcendentals=0),
        name="join",
    )(core.reshape(1), near, far)


CHUNKS = 2


def solution(mesh):
    tok_spec = P("dp", None, None)
    col_spec = P(None, "tp")
    row_spec = P("tp", None)
    n_dp = mesh.shape["dp"]
    core_swap = [(i, i ^ 1) for i in range(n_dp)]
    chip_swap = [(i, (i + 2) % n_dp) for i in range(n_dp)]
    cores = [[i, i + 1] for i in range(0, n_dp, 2)]

    def per_device(x_in, dy_in, positions, g_attn, q_gain, k_gain, w_q, w_k, w_v, w_o):
        _, n_seq, n_dim = x_in.shape
        dim = q_gain.shape[0]
        n_kv = w_k.shape[1] // dim
        group = w_q.shape[1] // w_k.shape[1]
        core = lax.rem(lax.axis_index("dp"), 2)
        chip = lax.div(lax.axis_index("dp"), 2)
        tp = lax.axis_index("tp")
        size = n_kv // CHUNKS
        own = []
        for c in range(CHUNKS):
            w_cat = interleave(w_q, w_k, w_v, range(c * size, (c + 1) * size), group, dim)
            own.append((w_cat, w_o[c * size * group * dim:(c + 1) * size * group * dim]))
        near = [(fetch_half(w_cat, core), fetch_half(w_out, core)) for w_cat, w_out in own]

        x_f32 = x_in.astype(jnp.float32).reshape(-1, n_dim)
        inv_rms = lax.rsqrt(jnp.mean(x_f32 * x_f32, axis=-1, keepdims=True) + EPS)
        x_hat = x_f32 * inv_rms
        normed = (x_hat * g_attn.astype(jnp.float32)).astype(jnp.bfloat16)
        dy_flat = dy_in.reshape(-1, n_dim)
        inv_freq = ROPE_THETA ** (-jnp.arange(0, dim, 2, dtype=jnp.float32) / dim)
        angles = positions.astype(jnp.float32).reshape(-1, 1) * inv_freq
        cos, sin = jnp.cos(angles), jnp.sin(angles)
        q_gain_f32 = q_gain.astype(jnp.float32).reshape(1, dim)
        k_gain_f32 = k_gain.astype(jnp.float32).reshape(1, dim)

        def heads(w_cat, w_out):
            qkv = dot_nn(normed, w_cat).astype(jnp.bfloat16)
            d_out = dot_nt(dy_flat, w_out).astype(jnp.bfloat16)
            return attention(qkv, d_out, cos, sin, q_gain_f32, k_gain_f32, n_seq, group, dim)

        def reduce_dp(part):
            part = lax.psum_scatter(part, "dp", scatter_dimension=0, axis_index_groups=cores, tiled=True)
            half = part.shape[0] // 2
            keep = lax.dynamic_slice_in_dim(part, chip * half, half, 0)
            send = lax.dynamic_slice_in_dim(part, (1 - chip) * half, half, 0)
            got = lax.ppermute(send, "dp", chip_swap)
            keep = keep + got
            got = lax.ppermute(keep, "dp", chip_swap)
            part = lax.dynamic_update_slice_in_dim(part, keep, chip * half, 0)
            part = lax.dynamic_update_slice_in_dim(part, got, (1 - chip) * half, 0)
            return lax.all_gather(part, "dp", axis_index_groups=cores, axis=0, tiled=True)

        def sums(o, d, w_cat, w_out, a_sum, d_sum):
            a_part = dot_nn(o, w_out)
            a_sum = a_part if a_sum is None else a_sum + a_part
            d_part = dot_nt(d, w_cat)
            d_sum = d_part if d_sum is None else d_sum + d_part
            return a_sum, d_sum

        dw_cat, dw_out, gq, gk = [], [], 0.0, 0.0
        a_own = d_own = a_far = d_far = None
        for w_cat, w_out in own:
            o, d, gq_part, gk_part = heads(w_cat, w_out)
            gq += jnp.sum(gq_part.reshape(-1, size, dim), axis=(0, 1))
            gk += jnp.sum(gk_part.reshape(-1, size, dim), axis=(0, 1))
            dw = dot_tn(normed, d)
            dw_cat.append(reduce_dp(dw))
            dw = dot_tn(o, dy_flat)
            dw_out.append(reduce_dp(dw))
            a_own, d_own = sums(o, d, w_cat, w_out, a_own, d_own)
        for c, (w_near, o_near) in enumerate(near):
            w_cat = join_halves(w_near, core, core_swap)
            w_out = join_halves(o_near, core, core_swap)
            o, d, _, _ = heads(w_cat, w_out)
            a_far, d_far = sums(o, d, w_cat, w_out, a_far, d_far)
            if c + 1 < CHUNKS:
                a_far, d_far = lax.optimization_barrier((a_far, d_far))

        y_out = (x_f32 + (a_own + a_far)).astype(jnp.bfloat16).reshape(x_in.shape)
        d_sum = d_own + d_far
        d_scaled = d_sum * g_attn.astype(jnp.float32)
        dx_f32 = dy_flat.astype(jnp.float32) + inv_rms * (d_scaled - x_hat * jnp.mean(d_scaled * x_hat, axis=-1, keepdims=True))
        dx_out = dx_f32.astype(jnp.bfloat16).reshape(x_in.shape)
        dg_part = jnp.sum(d_sum * x_hat, axis=0)
        mine = (jnp.arange(n_dim) < n_dim // 2) == (tp == 0)
        dg_part = jnp.where(mine, dg_part, 0.0)
        small = lax.psum(jnp.concatenate([gq, gk, dg_part]), ("tp", "dp"))

        wide = (group + 2) * dim

        def columns(start, stop):
            return jnp.concatenate([t[:, h * wide + start * dim:h * wide + stop * dim] for t in dw_cat for h in range(size)], axis=1)

        dw_q, dw_k, dw_v = columns(0, group), columns(group, group + 1), columns(group + 1, group + 2)
        dw_o = jnp.concatenate(dw_out, axis=0)
        return y_out, dx_out, dw_q, dw_k, dw_v, dw_o, small[:dim], small[dim:2 * dim], small[2 * dim:]

    return jax.shard_map(per_device, mesh=mesh, in_specs=(tok_spec, tok_spec, P("dp", None), P(), P(), P(), col_spec, col_spec, col_spec, row_spec), out_specs=(tok_spec, tok_spec, col_spec, col_spec, col_spec, row_spec, P(), P(), P()), check_vma=False)
```

time: 5760 us -> 3220 us (0.56)
  waiting for transfers between devices: 3850 us -> 1100 us
  Pallas kernels: 0 us -> 285 us
  local copies, waits for them, and re-layouts: 387 us -> 144 us
  matrix products: 1030 us -> 1180 us
    psum x2 -> x0, waiting for transfers between devices: 3850 us -> none  [the longest x1 2430 us: per_device(): lax.psum(jnp.dot(o_flat, w_o, preferred_element_type=jnp.float32), 'tp')]
    ppermute x0 -> x16, waiting for transfers between devices: none -> 1100 us  [the longest x4 734 us: fetch_half(): return lax.ppermute(send, 'tp', SWAP_TP)]
    pallas_call x0 -> x8, Pallas kernels: none -> 285 us  [the longest x4 208 us: attention(): pl.pallas_call(functools.partial(attend, group, dim), grid=(rows, kv), in...]
    unnamed x78 -> x55, local copies, waits for them, and re-layouts: 193 us -> 28.7 us
    dot_general x18 -> x20, matrix products: 1030 us -> 1180 us  [the longest x8 475 us: dot_nn(): return jnp.dot(a, b, preferred_element_type=jnp.float32)]
    another operation x4 -> x0, local copies, waits for them, and re-layouts: 86.7 us -> none  [the longest x2 68.5 us: attention_pair(): do_grp = d_out.reshape(n_batch, n_seq, n_kv, group_size, head_dim)]
    sub x1 -> x0, other arithmetic: 66.2 us -> none  [attention_pair(): attn_prob = jax.nn.softmax(jnp.where(causal, scores, -jnp.inf), axis=-1)]
    concatenate x0 -> x4, other arithmetic: none -> 65.3 us  [the longest x2 41.6 us: columns(): jnp.concatenate([t[:, h * wide + start * dim:h * wide + stop * dim] for t...]
  transfers between devices with their start and end apart: 2 -> 24, of which waited for: 2 -> 9; matrix products, arithmetic and copies ran while one was open for 6% -> 46% of each run, Pallas kernels for 0% -> 7%
where the time goes in v1:
time: 3220 us; the launch traced here: 3210 us
  matrix products  1180 us (37%)
  waiting for transfers between devices  1100 us (34%)
  other arithmetic  450 us (14%)
  Pallas kernels  285 us (9%)
  local copies, waits for them, and re-layouts  144 us (4%)
    ppermute x4, waiting for transfers between devices, fetch_half(): return lax.ppermute(send, 'tp', SWAP_TP)  734 us
    dot_general x8, matrix products, dot_nn(): return jnp.dot(a, b, preferred_element_type=jnp.float32)  475 us
    dot_general x8, matrix products, dot_nt(): return jnp.einsum('td,id->ti', a, b, preferred_element_type=jnp.float32)  462 us
    dot_general x4, matrix products, dot_tn(): return jnp.einsum('td,ti->di', a, b, preferred_element_type=jnp.float32)  240 us
    pallas_call x4, Pallas kernels, attention(): pl.pallas_call(functools.partial(attend, group, dim), grid=(rows, kv), in...  208 us
    ppermute x4, waiting for transfers between devices, reduce_dp(): got = lax.ppermute(keep, 'dp', chip_swap)  185 us
    ppermute x4, waiting for transfers between devices, reduce_dp(): got = lax.ppermute(send, 'dp', chip_swap)  182 us
    convert_element_type x1, other arithmetic, per_device(): dx_out = dx_f32.astype(jnp.bfloat16).reshape(x_in.shape)  135 us
  transfers between devices with their start and end apart: 24, of which 9 were waited for; matrix products, arithmetic and copies ran while one was open for 46% of the time, Pallas kernels for 7%

profile of v1, /device:TPU:0, one launch (start us, length us, event | category | flops | bytes accessed | tf_op | source)
XLA Modules:
  0.0 3214.1 jit_solution(5349467847214908376)
XLA Ops:
  24.3 21.9 fusion.4
  75.8 74.9 %convolution_convert_fusion.2.qkv_ref = bf16[4096,2048]{1,0:T(8,128)(2,1)} fusion(bf16[4096,3840]{1,0:T(8,128)(2,1)} %fusion.4, bf16[3840,2048]{1,0:T(8,128)(2,1)} %get-tuple-element.68), kind=kOutput, calls=%fused_computation.23 | convolution fusion | flops 64432898048 | bytes 63963136 | tf_op jit(solution)/shard_map/dot_general | solution.py:140
  150.7 40.2 %convolution_convert_fusion.4.do_ref = bf16[4096,1024]{1,0:T(8,128)(2,1)} fusion(bf16[4096,3840]{1,0:T(8,128)(2,1)} %bitcast.88, bf16[2048,3840]{1,0:T(8,128)(2,1)} %param.19), kind=kOutput, calls=%fused_computation.31 | convolution fusion | flops 32216449024 | bytes 47710208 | tf_op jit(solution)/shard_map/td,id->ti/dot_general | solution.py:144
  190.9 52.3 %attend.5 = (bf16[4096,1024]{1,0:T(8,128)(2,1)}, bf16[4096,2048]{1,0:T(8,128)(2,1)}, f32[64,512]{1,0:T(8,128)S(1)}, f32[64,512]{1,0:T(8,128)S(1)}) custom-call(bf16[4096,2048]{1,0:T(8,128)(2,1)} %convolution_convert_fusion.2.qkv_ref, bf16[4096,1024]{1,0:T(8,128)(2,1)} %convolution_convert_fusion.4.do_ref, f32[4096,128]{1,0:T(8,128)S(1)} %copy-done, ...), custom_call_target="tpu_custom_call" | custom-call | flops 19327352832 | bytes 50331648 | tf_op jit(solution)/shard_map/attend/pallas_call | solution.py:102
  243.2 42.3 %fusion.36 = f32[1024,3840]{1,0:T(8,128)} fusion(bf16[4096,1024]{1,0:T(8,128)(2,1)} %get-tuple-element.24, bf16[4096,3840]{1,0:T(8,128)(2,1)} %bitcast.89), kind=kOutput, calls=%fused_computation.92 | convolution fusion | flops 32212254720 | bytes 55574528 | tf_op jit(solution)/shard_map/td,ti->di/dot_general | solution.py:148
  285.6 40.1 %convolution_convert_fusion.5.do_ref = bf16[4096,1024]{1,0:T(8,128)(2,1)} fusion(bf16[4096,3840]{1,0:T(8,128)(2,1)} %bitcast.90, bf16[2048,3840]{1,0:T(8,128)(2,1)} %param.19), kind=kOutput, calls=%fused_computation.32 | convolution fusion | flops 32216449024 | bytes 47710208 | tf_op jit(solution)/shard_map/td,id->ti/dot_general | solution.py:144
  325.7 74.7 %convolution_convert_fusion.3.qkv_ref = bf16[4096,2048]{1,0:T(8,128)(2,1)} fusion(bf16[4096,3840]{1,0:T(8,128)(2,1)} %fusion.4, bf16[3840,2048]{1,0:T(8,128)(2,1)} %get-tuple-element.69), kind=kOutput, calls=%fused_computation.24 | convolution fusion | flops 64432898048 | bytes 63963136 | tf_op jit(solution)/shard_map/dot_general | solution.py:140
  402.0 51.8 %attend.4 = (bf16[4096,1024]{1,0:T(8,128)(2,1)}, bf16[4096,2048]{1,0:T(8,128)(2,1)}, f32[64,512]{1,0:T(8,128)S(1)}, f32[64,512]{1,0:T(8,128)S(1)}) custom-call(bf16[4096,2048]{1,0:T(8,128)(2,1)} %convolution_convert_fusion.3.qkv_ref, bf16[4096,1024]{1,0:T(8,128)(2,1)} %convolution_convert_fusion.5.do_ref, f32[4096,128]{1,0:T(8,128)S(1)} %copy-done.1, ...), custom_call_target="tpu_custom_call" | custom-call | flops 19327352832 | bytes 50331648 | tf_op jit(solution)/shard_map/attend/pallas_call | solution.py:102
  453.8 42.5 %fusion.35 = f32[1024,3840]{1,0:T(8,128)} fusion(bf16[4096,1024]{1,0:T(8,128)(2,1)} %get-tuple-element.23, bf16[4096,3840]{1,0:T(8,128)(2,1)} %bitcast.91), kind=kOutput, calls=%fused_computation.91 | convolution fusion | flops 32212254720 | bytes 55574528 | tf_op jit(solution)/shard_map/td,ti->di/dot_general | solution.py:148
  496.4 75.8 %fusion.34 = f32[3840,2048]{1,0:T(8,128)} fusion(bf16[4096,3840]{1,0:T(8,128)(2,1)} %fusion.4, bf16[4096,2048]{1,0:T(8,128)(2,1)} %get-tuple-element.30), kind=kOutput, calls=%fused_computation.90 | convolution fusion | flops 64424509440 | bytes 79691776 | tf_op jit(solution)/shard_map/td,ti->di/dot_general | solution.py:148
  572.3 13.4 dynamic-slice_convert_fusion.1
  590.2 79.6 %fusion.33 = f32[3840,2048]{1,0:T(8,128)} fusion(bf16[4096,3840]{1,0:T(8,128)(2,1)} %fusion.4, bf16[4096,2048]{1,0:T(8,128)(2,1)} %get-tuple-element.29), kind=kOutput, calls=%fused_computation.89 | convolution fusion | flops 64424509440 | bytes 79691776 | tf_op jit(solution)/shard_map/td,ti->di/dot_general | solution.py:148
  669.9 14.3 fusion.25
  692.1 15.6 dynamic-slice_convert_fusion
  715.9 76.0 %fusion.30 = f32[4096,3840]{1,0:T(8,128)} fusion(bf16[4096,2048]{1,0:T(8,128)(2,1)} %get-tuple-element.29, bf16[3840,2048]{1,0:T(8,128)(2,1)} %get-tuple-element.69), kind=kOutput, calls=%fused_computation.86 | convolution fusion | flops 64424509440 | bytes 95420416 | tf_op jit(solution)/shard_map/td,id->ti/dot_general | solution.py:144
  791.9 75.8 %fusion.31 = f32[4096,3840]{1,0:T(8,128)} fusion(bf16[4096,2048]{1,0:T(8,128)(2,1)} %get-tuple-element.30, bf16[3840,2048]{1,0:T(8,128)(2,1)} %get-tuple-element.68), kind=kOutput, calls=%fused_computation.87 | convolution fusion | flops 64424509440 | bytes 95420416 | tf_op jit(solution)/shard_map/td,id->ti/dot_general | solution.py:144
  867.8 229.9 %collective-permute-done.2.near_ref = f32[512,3840]{1,0:T(8,128)} collective-permute-done((f32[512,3840]{1,0:T(8,128)}, f32[512,3840]{1,0:T(8,128)}, u32[]{:S(2)}, u32[]{:S(2)}) %collective-permute-start.2) | collective-permute-done | bytes 7864352 | tf_op jit(solution)/shard_map/ppermute | solution.py:154
  1097.7 504.5 %collective-permute-done.6.near_ref = f32[512,3840]{1,0:T(8,128)} collective-permute-done((f32[512,3840]{1,0:T(8,128)}, f32[512,3840]{1,0:T(8,128)}, u32[]{:S(2)}, u32[]{:S(2)}) %collective-permute-start.6) | collective-permute-done | bytes 7864352 | tf_op jit(solution)/shard_map/ppermute | solution.py:154
  1602.2 42.4 %fusion.18 = f32[4096,3840]{1,0:T(8,128)} fusion(bf16[4096,1024]{1,0:T(8,128)(2,1)} %get-tuple-element.23, bf16[2048,3840]{1,0:T(8,128)(2,1)} %param.19), kind=kOutput, calls=%fused_computation.74 | convolution fusion | flops 32212254720 | bytes 79167488 | tf_op jit(solution)/shard_map/dot_general | solution.py:140
  1646.5 42.7 %fusion.15 = f32[4096,3840]{1,0:T(8,128)} fusion(bf16[4096,1024]{1,0:T(8,128)(2,1)} %get-tuple-element.24, bf16[2048,3840]{1,0:T(8,128)(2,1)} %param.19), kind=kOutput, calls=%fused_computation.71 | convolution fusion | flops 32212254720 | bytes 79167488 | tf_op jit(solution)/shard_map/dot_general | solution.py:140
  1717.6 40.2 %convert_bitcast_fusion.1.do_ref = bf16[4096,1024]{1,0:T(8,128)(2,1)} fusion(bf16[1024,3840]{1,0:T(8,128)(2,1)} %join.5, bf16[4096,3840]{1,0:T(8,128)(2,1)} %bitcast.92), kind=kOutput, calls=%fused_computation.26 | convolution fusion | flops 32216449024 | bytes 47710208 | tf_op jit(solution)/shard_map/td,id->ti/dot_general | solution.py:144
  1762.7 41.3 %collective-permute-done.14 = f32[256,3840]{1,0:T(8,128)} collective-permute-done((f32[256,3840]{1,0:T(8,128)}, f32[256,3840]{1,0:T(8,128)}, u32[]{:S(2)}, u32[]{:S(2)}) %collective-permute-start.14) | collective-permute-done | bytes 3932192 | tf_op jit(solution)/shard_map/ppermute | solution.py:242
  1812.7 37.7 %convert_bitcast_fusion.do_ref = bf16[4096,1024]{1,0:T(8,128)(2,1)} fusion(bf16[1024,3840]{1,0:T(8,128)(2,1)S(1)} %bitcast.101, bf16[4096,3840]{1,0:T(8,128)(2,1)} %bitcast.93), kind=kOutput, calls=%fused_computation.25 | convolution fusion | flops 32216449024 | bytes 47710208 | tf_op jit(solution)/shard_map/td,id->ti/dot_general | solution.py:144
  1850.5 27.4 join.4
  1897.0 75.5 %collective-permute-done.15 = f32[256,3840]{1,0:T(8,128)} collective-permute-done((f32[256,3840]{1,0:T(8,128)}, f32[256,3840]{1,0:T(8,128)}, u32[]{:S(2)}, u32[]{:S(2)}) %collective-permute-start.15) | collective-permute-done | bytes 3932192 | tf_op jit(solution)/shard_map/ppermute | solution.py:244
  1988.0 78.5 %convolution_convert_fusion.1.qkv_ref = bf16[4096,2048]{1,0:T(8,128)(2,1)} fusion(bf16[4096,3840]{1,0:T(8,128)(2,1)} %fusion.4, bf16[3840,2048]{1,0:T(8,128)(2,1)} %join.4), kind=kOutput, calls=%fused_computation.22 | convolution fusion | flops 64432898048 | bytes 63963136 | tf_op jit(solution)/shard_map/dot_general | solution.py:140
  2068.1 52.0 %attend.6 = (bf16[4096,1024]{1,0:T(8,128)(2,1)}, bf16[4096,2048]{1,0:T(8,128)(2,1)}, f32[64,512]{1,0:T(8,128)}, f32[64,512]{1,0:T(8,128)}) custom-call(bf16[4096,2048]{1,0:T(8,128)(2,1)} %convolution_convert_fusion.1.qkv_ref, bf16[4096,1024]{1,0:T(8,128)(2,1)} %convert_bitcast_fusion.1.do_ref, f32[4096,128]{1,0:T(8,128)S(1)} %copy-done.2, ...), custom_call_target="tpu_custom_call" | custom-call | flops 19327352832 | bytes 50331648 | tf_op jit(solution)/shard_map/attend/pallas_call | solution.py:102
  2124.4 100.5 %collective-permute-done.10 = f32[960,2048]{1,0:T(8,128)} collective-permute-done((f32[960,2048]{1,0:T(8,128)}, f32[960,2048]{1,0:T(8,128)}, u32[]{:S(2)}, u32[]{:S(2)}) %collective-permute-start.10) | collective-permute-done | bytes 7864352 | tf_op jit(solution)/shard_map/ppermute | solution.py:242
  2224.8 14.5 constant_dynamic-update-slice_fusion.5
  2241.2 76.2 %fusion.28 = f32[4096,3840]{1,0:T(8,128)} fusion(bf16[4096,2048]{1,0:T(8,128)(2,1)} %get-tuple-element.26, bf16[3840,2048]{1,0:T(8,128)(2,1)} %join.4), kind=kOutput, calls=%fused_computation.84 | convolution fusion | flops 64424509440 | bytes 95420416 | tf_op jit(solution)/shard_map/td,id->ti/dot_general | solution.py:144
  2317.4 27.4 join.6
  2352.4 59.3 %collective-permute-done.11 = f32[960,2048]{1,0:T(8,128)} collective-permute-done((f32[960,2048]{1,0:T(8,128)}, f32[960,2048]{1,0:T(8,128)}, u32[]{:S(2)}, u32[]{:S(2)}) %collective-permute-start.11) | collective-permute-done | bytes 7864352 | tf_op jit(solution)/shard_map/ppermute | solution.py:244
  2419.2 76.5 %convolution_convert_fusion.qkv_ref = bf16[4096,2048]{1,0:T(8,128)(2,1)} fusion(bf16[4096,3840]{1,0:T(8,128)(2,1)} %fusion.4, bf16[3840,2048]{1,0:T(8,128)(2,1)} %join.6), kind=kOutput, calls=%fused_computation.21 | convolution fusion | flops 64432898048 | bytes 63963136 | tf_op jit(solution)/shard_map/dot_general | solution.py:140
  2497.4 52.2 %attend.7 = (bf16[4096,1024]{1,0:T(8,128)(2,1)}, bf16[4096,2048]{1,0:T(8,128)(2,1)}, f32[64,512]{1,0:T(8,128)}, f32[64,512]{1,0:T(8,128)}) custom-call(bf16[4096,2048]{1,0:T(8,128)(2,1)} %convolution_convert_fusion.qkv_ref, bf16[4096,1024]{1,0:T(8,128)(2,1)} %convert_bitcast_fusion.do_ref, f32[4096,128]{1,0:T(8,128)S(1)} %copy-done.3, ...), custom_call_target="tpu_custom_call" | custom-call | flops 19327352832 | bytes 50331648 | tf_op jit(solution)/shard_map/attend/pallas_call | solution.py:102
  2549.5 29.5 collective-permute-done.8
  2579.0 14.6 constant_dynamic-update-slice_fusion.7
  2595.2 75.6 %fusion.32 = f32[4096,3840]{1,0:T(8,128)} fusion(bf16[4096,2048]{1,0:T(8,128)(2,1)} %get-tuple-element.32, bf16[3840,2048]{1,0:T(8,128)(2,1)} %join.6), kind=kOutput, calls=%fused_computation.88 | convolution fusion | flops 64424509440 | bytes 95420416 | tf_op jit(solution)/shard_map/td,id->ti/dot_general | solution.py:144
  2670.8 42.6 %fusion.27 = f32[4096,3840]{1,0:T(8,128)} fusion(bf16[4096,1024]{1,0:T(8,128)(2,1)} %get-tuple-element.25, bf16[1024,3840]{1,0:T(8,128)(2,1)} %join.5), kind=kOutput, calls=%fused_computation.83 | convolution fusion | flops 32212254720 | bytes 79167488 | tf_op jit(solution)/shard_map/dot_general | solution.py:140
  2713.5 50.4 %collective-permute-done.9 = f32[960,2048]{1,0:T(8,128)} collective-permute-done((f32[960,2048]{1,0:T(8,128)}, f32[960,2048]{1,0:T(8,128)}, u32[]{:S(2)}, u32[]{:S(2)}) %collective-permute-start.9) | collective-permute-done | bytes 7864352 | tf_op jit(solution)/shard_map/ppermute | solution.py:244
  2771.3 119.9 %fusion.10 = (f32[3840]{0:T(1024)S(1)}, f32[4096]{0:T(1024)S(1)}, f32[4096,3840]{1,0:T(8,128)}) fusion(bf16[8,512,3840]{2,1,0:T(8,128)(2,1)} %param.10, f32[4096]{0:T(1024)S(1)} %bitcast.103, f32[3840]{0:T(1024)S(1)} %copy-done.11, f32[4096,3840]{1,0:T(8,128)} %fusion.28, f32[4096,3840]{1,0:T(8,128)} %fusion.32, f32[4096,3840]{1,0:T(8,128)} %fusion.30, ...), kind=kLoop, calls=%fused_computation.13 | loop fusion | flops 157278464 | bytes 346093568 | tf_op jit(solution)/shard_map/reduce_sum | solution.py:280
  2891.2 23.6 psum.7
  2916.0 42.2 %fusion.29 = f32[4096,3840]{1,0:T(8,128)} fusion(bf16[4096,1024]{1,0:T(8,128)(2,1)} %get-tuple-element.28, bf16[1024,3840]{1,0:T(8,128)(2,1)} %join.7), kind=kOutput, calls=%fused_computation.85 | convolution fusion | flops 32212254720 | bytes 79167488 | tf_op jit(solution)/shard_map/dot_general | solution.py:140
  2958.2 134.8 %fusion.9 = (bf16[4096,3840]{1,0:T(8,128)(2,1)}, bf16[4096,3840]{1,0:T(8,128)(2,1)}) fusion(bf16[8,512,3840]{2,1,0:T(8,128)(2,1)} %param.10, f32[4096,3840]{1,0:T(8,128)} %get-tuple-element.47, f32[4096]{0:T(1024)S(1)} %broadcast_multiply_fusion, f32[3840]{0:T(1024)S(1)} %copy-done.11, f32[4096]{0:T(1024)S(1)} %bitcast.104, bf16[8,512,3840]{2,1,0:T(8,128)(2,1)} %param.11, ...), kind=kLoop, calls=%fused_computation.12 | loop fusion | flops 220200960 | bytes 440450048 | tf_op jit(solution)/shard_map/convert_element_type | solution.py:279
  3093.1 23.7 pad_maximum_fusion.1
  3116.8 13.2 fusion.24
  3130.1 12.8 fusion.23
  3142.9 21.1 pad_maximum_fusion
  3186.6 20.4 pad_maximum_fusion.2
  (150 shorter events, 205.0 us)
Async XLA Ops:
  7.2 1704.4 %reduce-scatter.11.cloned.1.call-start = ((), (), s32[]{:S(2)}) async-start(), calls=%async_computation.10 | async-start | bytes 23592960 | tf_op jit(solution)/shard_map/reduce_scatter | solution.py:238
  7.2 11.3 copy-start.13
  18.5 5.8 copy-start.12
  18.5 5.8 copy-start.16
  18.5 5.8 copy-start.17
  18.6 27.6 copy-start.8
  18.6 27.6 copy-start.10
  24.3 166.6 %copy-start.4 = (f32[256]{0:T(256)}, f32[256]{0:T(256)S(1)}, u32[]{:S(2)}) copy-start(f32[256]{0:T(256)S(1)} %reshape.94) | copy-start | bytes 3076
  24.3 166.6 %copy-start.6 = (f32[256]{0:T(256)}, f32[256]{0:T(256)S(1)}, u32[]{:S(2)}) copy-start(f32[256]{0:T(256)S(1)} %reshape.96) | copy-start | bytes 3076
  46.2 15.5 slice-start
  50.7 13.3 slice-start.2
  55.2 6.7 slice-start.1
  55.2 9.2 slice-start.3
  150.7 40.2 %copy-start = (f32[4096,128]{1,0:T(8,128)S(1)}, f32[4096,128]{1,0:T(8,128)}, u32[]{:S(2)}) copy-start(f32[4096,128]{1,0:T(8,128)} %get-tuple-element.79.cos_ref) | copy-start | bytes 6291460
  285.5 1472.2 %reduce-scatter.9.cloned.1.call-start = ((), (), s32[]{:S(2)}) async-start(), calls=%async_computation.8 | async-start | bytes 23592960 | tf_op jit(solution)/shard_map/reduce_scatter | solution.py:238
  325.7 74.7 %copy-start.5 = (f32[256]{0:T(256)S(1)}, f32[256]{0:T(256)}, u32[]{:S(2)}) copy-start(f32[256]{0:T(256)} %copy-done.4) | copy-start | bytes 3076
  325.7 74.7 %copy-start.7 = (f32[256]{0:T(256)S(1)}, f32[256]{0:T(256)}, u32[]{:S(2)}) copy-start(f32[256]{0:T(256)} %copy-done.6) | copy-start | bytes 3076
  400.4 1.6 copy-start.1
  496.4 1480.5 %reduce-scatter.7.cloned.1.call-start = ((), (), s32[]{:S(2)}) async-start(), calls=%async_computation.6 | async-start | bytes 47185920 | tf_op jit(solution)/shard_map/reduce_scatter | solution.py:238
  572.2 1772.5 %reduce-scatter.5.cloned.1.call-start = ((), (), s32[]{:S(2)}) async-start(), calls=%async_computation.4 | async-start | bytes 47185920 | tf_op jit(solution)/shard_map/reduce_scatter | solution.py:238
  585.7 1060.3 %collective-permute-start = (f32[1920,2048]{1,0:T(8,128)}, f32[1920,2048]{1,0:T(8,128)}, u32[]{:S(2)}, u32[]{:S(2)}) collective-permute-start(f32[1920,2048]{1,0:T(8,128)} %dynamic-slice_convert_fusion.1), channel_id=1, source_target_pairs={{0,4},{4,0},{1,5},{5,1},{2,6},{6,2},{3,7},{7,3}} | collective-permute-start | bytes 47185928 | tf_op jit(solution)/shard_map/ppermute | solution.py:154
  669.8 2423.2 %all-gather.11.cloned.1.call-start = ((), (), s32[]{:S(2)}) async-start(), calls=%async_computation.11 | async-start | bytes 23592960 | tf_op jit(solution)/shard_map/all_gather | solution.py:247
  692.1 405.6 %collective-permute-start.2 = (f32[512,3840]{1,0:T(8,128)}, f32[512,3840]{1,0:T(8,128)}, u32[]{:S(2)}, u32[]{:S(2)}) collective-permute-start(f32[512,3840]{1,0:T(8,128)} %dynamic-slice_convert_fusion.3), channel_id=1, source_target_pairs={{0,4},{4,0},{1,5},{5,1},{2,6},{6,2},{3,7},{7,3}} | collective-permute-start | bytes 23592968 | tf_op jit(solution)/shard_map/ppermute | solution.py:154
  707.7 981.4 %collective-permute-start.4 = (f32[1920,2048]{1,0:T(8,128)}, f32[1920,2048]{1,0:T(8,128)}, u32[]{:S(2)}, u32[]{:S(2)}) collective-permute-start(f32[1920,2048]{1,0:T(8,128)} %dynamic-slice_convert_fusion), channel_id=1, source_target_pairs={{0,4},{4,0},{1,5},{5,1},{2,6},{6,2},{3,7},{7,3}} | collective-permute-start | bytes 47185928 | tf_op jit(solution)/shard_map/ppermute | solution.py:154
  715.7 886.5 %collective-permute-start.6 = (f32[512,3840]{1,0:T(8,128)}, f32[512,3840]{1,0:T(8,128)}, u32[]{:S(2)}, u32[]{:S(2)}) collective-permute-start(f32[512,3840]{1,0:T(8,128)} %dynamic-slice_convert_fusion.2), channel_id=1, source_target_pairs={{0,4},{4,0},{1,5},{5,1},{2,6},{6,2},{3,7},{7,3}} | collective-permute-start | bytes 23592968 | tf_op jit(solution)/shard_map/ppermute | solution.py:154
  1097.7 591.5 %collective-permute-start.3 = (f32[512,3840]{1,0:T(8,128)}, f32[512,3840]{1,0:T(8,128)}, u32[]{:S(2)}, u32[]{:S(2)}) collective-permute-start(f32[512,3840]{1,0:T(8,128)} %collective-permute-done.2.near_ref), channel_id=1, source_target_pairs={{0,1},{1,0},{2,3},{3,2},{4,5},{5,4},{6,7},{7,6}} | collective-permute-start | bytes 23592968 | tf_op jit(solution)/shard_map/ppermute | solution.py:173
  1602.2 98.2 %collective-permute-start.7 = (f32[512,3840]{1,0:T(8,128)}, f32[512,3840]{1,0:T(8,128)}, u32[]{:S(2)}, u32[]{:S(2)}) collective-permute-start(f32[512,3840]{1,0:T(8,128)} %collective-permute-done.6.near_ref), channel_id=1, source_target_pairs={{0,1},{1,0},{2,3},{3,2},{4,5},{5,4},{6,7},{7,6}} | collective-permute-start | bytes 23592968 | tf_op jit(solution)/shard_map/ppermute | solution.py:173
  1646.0 204.5 %collective-permute-start.1 = (f32[1920,2048]{1,0:T(8,128)}, f32[1920,2048]{1,0:T(8,128)}, u32[]{:S(2)}, u32[]{:S(2)}) collective-permute-start(f32[1920,2048]{1,0:T(8,128)} %collective-permute-done.near_ref), channel_id=1, source_target_pairs={{0,1},{1,0},{2,3},{3,2},{4,5},{5,4},{6,7},{7,6}} | collective-permute-start | bytes 47185928 | tf_op jit(solution)/shard_map/ppermute | solution.py:173
  1689.1 628.2 %collective-permute-start.5 = (f32[1920,2048]{1,0:T(8,128)}, f32[1920,2048]{1,0:T(8,128)}, u32[]{:S(2)}, u32[]{:S(2)}) collective-permute-start(f32[1920,2048]{1,0:T(8,128)} %collective-permute-done.4.near_ref), channel_id=1, source_target_pairs={{0,1},{1,0},{2,3},{3,2},{4,5},{5,4},{6,7},{7,6}} | collective-permute-start | bytes 47185928 | tf_op jit(solution)/shard_map/ppermute | solution.py:173
  1715.9 88.1 %collective-permute-start.14 = (f32[256,3840]{1,0:T(8,128)}, f32[256,3840]{1,0:T(8,128)}, u32[]{:S(2)}, u32[]{:S(2)}) collective-permute-start(f32[256,3840]{1,0:T(8,128)} %constant_dynamic-slice_fusion), channel_id=1, source_target_pairs={{0,2},{1,3},{2,0},{3,1},{4,6},{5,7},{6,4},{7,5}} | collective-permute-start | bytes 11796488 | tf_op jit(solution)/shard_map/ppermute | solution.py:242
  1757.8 54.9 %slice-start.4 = ((s8[7864320]{0:T(1024)(128)(4,1)}), s8[4194304]{0:T(1024)(128)(4,1)S(1)}, s32[]{:S(2)}) async-start(s8[7864320]{0:T(1024)(128)(4,1)} %bitcast.100), calls=%async_computation.16 | async-start | bytes 8388608
  1762.4 50.3 %slice-start.5 = ((s8[7864320]{0:T(1024)(128)(4,1)}), s8[3670016]{0:T(1024)(128)(4,1)S(1)}, s32[]{:S(2)}) async-start(s8[7864320]{0:T(1024)(128)(4,1)} %bitcast.100), calls=%async_computation.17 | async-start | bytes 7340032
  1762.4 125.9 %collective-permute-start.12 = (f32[256,3840]{1,0:T(8,128)}, f32[256,3840]{1,0:T(8,128)}, u32[]{:S(2)}, u32[]{:S(2)}) collective-permute-start(f32[256,3840]{1,0:T(8,128)} %constant_dynamic-slice_fusion.1), channel_id=1, source_target_pairs={{0,2},{1,3},{2,0},{3,1},{4,6},{5,7},{6,4},{7,5}} | collective-permute-start | bytes 11796488 | tf_op jit(solution)/shard_map/ppermute | solution.py:242
  1811.0 161.5 %collective-permute-start.15 = (f32[256,3840]{1,0:T(8,128)}, f32[256,3840]{1,0:T(8,128)}, u32[]{:S(2)}, u32[]{:S(2)}) collective-permute-start(f32[256,3840]{1,0:T(8,128)} %get-tuple-element.42), channel_id=1, source_target_pairs={{0,2},{1,3},{2,0},{3,1},{4,6},{5,7},{6,4},{7,5}} | collective-permute-start | bytes 11796488 | tf_op jit(solution)/shard_map/ppermute | solution.py:244
  1895.2 224.9 %collective-permute-start.13 = (f32[256,3840]{1,0:T(8,128)}, f32[256,3840]{1,0:T(8,128)}, u32[]{:S(2)}, u32[]{:S(2)}) collective-permute-start(f32[256,3840]{1,0:T(8,128)} %get-tuple-element.40), channel_id=1, source_target_pairs={{0,2},{1,3},{2,0},{3,1},{4,6},{5,7},{6,4},{7,5}} | collective-permute-start | bytes 11796488 | tf_op jit(solution)/shard_map/ppermute | solution.py:244
  1976.8 1116.3 %all-gather.9.cloned.1.call-start = ((), (), s32[]{:S(2)}) async-start(), calls=%async_computation.9 | async-start | bytes 23592960 | tf_op jit(solution)/shard_map/all_gather | solution.py:247
  1986.3 238.6 %collective-permute-start.10 = (f32[960,2048]{1,0:T(8,128)}, f32[960,2048]{1,0:T(8,128)}, u32[]{:S(2)}, u32[]{:S(2)}) collective-permute-start(f32[960,2048]{1,0:T(8,128)} %constant_dynamic-slice_fusion.2), channel_id=1, source_target_pairs={{0,2},{1,3},{2,0},{3,1},{4,6},{5,7},{6,4},{7,5}} | collective-permute-start | bytes 23592968 | tf_op jit(solution)/shard_map/ppermute | solution.py:242
  2066.5 1.6 copy-start.2
  2124.3 992.5 %all-gather.7.cloned.1.call-start = ((), (), s32[]{:S(2)}) async-start(), calls=%async_computation.7 | async-start | bytes 47185920 | tf_op jit(solution)/shard_map/all_gather | solution.py:247
  2239.3 172.4 %collective-permute-start.11 = (f32[960,2048]{1,0:T(8,128)}, f32[960,2048]{1,0:T(8,128)}, u32[]{:S(2)}, u32[]{:S(2)}) collective-permute-start(f32[960,2048]{1,0:T(8,128)} %get-tuple-element.46), channel_id=1, source_target_pairs={{0,2},{1,3},{2,0},{3,1},{4,6},{5,7},{6,4},{7,5}} | collective-permute-start | bytes 23592968 | tf_op jit(solution)/shard_map/ppermute | solution.py:244
  2352.2 226.8 %collective-permute-start.8 = (f32[960,2048]{1,0:T(8,128)}, f32[960,2048]{1,0:T(8,128)}, u32[]{:S(2)}, u32[]{:S(2)}) collective-permute-start(f32[960,2048]{1,0:T(8,128)} %constant_dynamic-slice_fusion.3), channel_id=1, source_target_pairs={{0,2},{1,3},{2,0},{3,1},{4,6},{5,7},{6,4},{7,5}} | collective-permute-start | bytes 23592968 | tf_op jit(solution)/shard_map/ppermute | solution.py:242
  2419.2 710.9 %all-gather.5.cloned.1.call-start = ((), (), s32[]{:S(2)}) async-start(), calls=%async_computation.5 | async-start | bytes 47185920 | tf_op jit(solution)/shard_map/all_gather | solution.py:247
  2495.8 1.6 copy-start.3
  2593.6 170.3 %collective-permute-start.9 = (f32[960,2048]{1,0:T(8,128)}, f32[960,2048]{1,0:T(8,128)}, u32[]{:S(2)}, u32[]{:S(2)}) collective-permute-start(f32[960,2048]{1,0:T(8,128)} %get-tuple-element.44), channel_id=1, source_target_pairs={{0,2},{1,3},{2,0},{3,1},{4,6},{5,7},{6,4},{7,5}} | collective-permute-start | bytes 23592968 | tf_op jit(solution)/shard_map/ppermute | solution.py:244
  2763.8 7.4 copy-start.9
  2763.8 7.4 copy-start.11
  2771.2 120.0 %copy-start.14 = (f32[256]{0:T(256)S(1)}, f32[256]{0:T(256)}, u32[]{:S(2)}) copy-start(f32[256]{0:T(256)} %add.117) | copy-start | bytes 3076
  2771.2 120.0 %copy-start.15 = (f32[256]{0:T(256)S(1)}, f32[256]{0:T(256)}, u32[]{:S(2)}) copy-start(f32[256]{0:T(256)} %add.116) | copy-start | bytes 3076
Sparse Core Ops, SparseCore 0:
  285.7 25.8 reduce-scatter.10
  496.5 26.2 reduce-scatter.8
  572.3 46.0 reduce-scatter.6
  670.0 41.8 reduce-scatter.4
  1976.9 26.9 all-gather.10
  2124.4 25.7 all-gather.8
  2419.3 47.0 all-gather.6
  2771.3 46.9 all-gather.4
